TPU v7x, 32 devices: a whole 2x2x4 slice. The times are simulated.
32 devices in a mesh: row: 4 (over z), col: 4 (over y, x), layer: 2 (over core).
Axes of the slice: x: 2, y: 2, z: 4, core: 2. Of those that a mesh axis runs over, the one named last changes fastest.
Arguments:
- wavefunction: float32 [4096, 4096], P('row', 'col'), may hold values from -0.015625 to 1.515625
- start_block: float32 [4096, 2048], P(('col', 'layer'), 'row'), may hold values from -6 to 6
Outputs:
- basis: float32 [4096, 2048], P(('col', 'layer'), 'row')
All inputs are finite; a program needn't handle non-finite values.
Results may differ from a plain program's by a relative error of at most 0.0003.
Values sent between devices are 32-bit elements; how exact they have to be, the bound alone decides.
No kernel may reach another device: no remote copies, remote signals or barrier semaphores. Data moves between devices by JAX's collectives and lax.ppermute only.
A program may use at most 128 MiB of HBM per device.

v0:
```python
import math
import jax
import jax.numpy as jnp
from jax import lax
from jax.sharding import PartitionSpec as P


def spread(x, axis, root):
    mine = lax.axis_index(axis) == root
    return lax.psum(jnp.where(mine, x, jnp.zeros_like(x)), axis)


def cross(left, right):
    return lax.dot_general(
        left,
        right,
        (((0,), (0,)), ((), ())),
        precision=lax.Precision.HIGHEST,
        preferred_element_type=jnp.float32,
    )


def times(left, right):
    return jnp.dot(left, right, precision=lax.Precision.HIGHEST, preferred_element_type=jnp.float32)


def apply_density(rho_slab, basis_block):
    return lax.psum_scatter(
        cross(rho_slab, basis_block), ("col", "layer"), scatter_dimension=0, tiled=True
    )


def orthonormalize(image_block):
    panel_owner = lax.axis_index("row")
    panels = lax.axis_size("row")
    current = image_block
    gram_matrix = lax.psum(cross(current, current), ("col", "layer"))
    for panel_index in range(panels):
        factor = jnp.linalg.cholesky(gram_matrix)
        new_basis = jax.scipy.linalg.solve_triangular(factor, current.T, lower=True).T
        current = jnp.where(panel_owner == panel_index, new_basis, current)
        if panel_index + 1 < panels:
            chosen = spread(current, "row", panel_index)
            later = panel_owner > panel_index
            correlation, square = lax.psum(
                (cross(chosen, current), cross(current, current)), ("col", "layer")
            )
            current = jnp.where(later, current - times(chosen, correlation), current)
            gram_matrix = jnp.where(later, square - cross(correlation, correlation), square)
    return current


def shards(wavefunction, start_block):
    layers = lax.axis_size("layer")
    column_width = wavefunction.shape[1] // layers
    own_slice = lax.dynamic_slice_in_dim(
        wavefunction, lax.axis_index("layer") * column_width, column_width, 1
    )
    own_rows = lax.all_gather(own_slice, "col", axis=1, tiled=True)
    partner = spread(own_rows, "row", lax.axis_index("col"))
    rho_part = lax.psum_scatter(
        lax.dot_general(
            partner,
            own_rows,
            (((1,), (1,)), ((), ())),
            precision=lax.Precision.HIGHEST,
            preferred_element_type=jnp.float32,
        ),
        "layer",
        scatter_dimension=0,
        tiled=True,
    )
    rho_slab = lax.all_gather(rho_part, "row", axis=1, tiled=True)
    current = start_block
    image_block = apply_density(rho_slab, current)
    current = orthonormalize(image_block)
    return current * math.sqrt(rho_slab.shape[1])


def solution(mesh):
    placed = (P("row", "col"), P(("col", "layer"), "row"))
    return jax.shard_map(
        shards, mesh=mesh, in_specs=placed, out_specs=P(("col", "layer"), "row"), check_vma=False
    )
```

profile of v0, /device:TPU:0, one launch (start us, length us, event | category | flops | bytes accessed | tf_op | source)
XLA Modules:
  0.0 1721.6 jit_solution(5460350467099761118)
XLA Ops:
  9.9 90.3 %all-gather.3.cloned.1.call-done = f32[1024,2048]{1,0:T(8,128)} async-done(((f32[1024,512]{1,0:T(8,128)}), f32[1024,2048]{1,0:T(8,128)}) %all-gather.3.cloned.1.call-update) | async-done | bytes 8388624 | tf_op jit(solution)/shard_map/all_gather | solution.py:59
  108.5 290.9 %all-reduce.13.cloned.1.call-done = f32[1024,2048]{1,0:T(8,128)} async-done(((f32[1024,2048]{1,0:T(8,128)}), f32[1024,2048]{1,0:T(8,128)}) %all-reduce.13.cloned.1.call-update) | async-done | bytes 8388624 | tf_op jit(solution)/shard_map/psum | solution.py:10
  399.4 32.1 %fusion.156 = f32[1024,1024]{1,0:T(8,128)} fusion(f32[1024,2048]{1,0:T(8,128)} %all-reduce.13.cloned.1.call-done, f32[1024,2048]{1,0:T(8,128)} %all-gather.3.cloned.1.call-done), kind=kOutput, calls=%fused_computation.284 | convolution fusion | flops 25769803776 | bytes 20971520 | tf_op jit(solution)/shard_map/dot_general | solution.py:62
  431.6 11.1 reduce-scatter.3.cloned.1.call-done
  443.1 152.0 %all-gather.5.cloned.1.call-done = f32[512,4096]{1,0:T(8,128)} async-done(((f32[512,1024]{1,0:T(8,128)}), f32[512,4096]{1,0:T(8,128)}) %all-gather.5.cloned.1.call-update) | async-done | bytes 8388624 | tf_op jit(solution)/shard_map/all_gather | solution.py:73
  595.1 17.1 fusion.157
  612.2 69.6 %reduce-scatter.5.cloned.1.call-done = f32[512,512]{0,1:T(8,128)} async-done(((f32[4096,512]{0,1:T(8,128)}), f32[512,512]{0,1:T(8,128)}) %reduce-scatter.5.cloned.1.call-update) | async-done | bytes 1048592 | tf_op jit(solution)/shard_map/reduce_scatter | solution.py:28
  686.9 56.3 %all-reduce.15.cloned.1.call-done = f32[512,512]{0,1:T(8,128)} async-done(((f32[512,512]{0,1:T(8,128)}), f32[512,512]{0,1:T(8,128)}) %all-reduce.15.cloned.1.call-update) | async-done | bytes 1048592 | tf_op jit(solution)/shard_map/psum | solution.py:37
  746.2 11.7 cholesky.462
  757.9 9.8 custom-call.35
  768.6 11.7 cholesky.481
  780.3 10.0 custom-call.36
  790.9 11.7 cholesky.502
  803.4 9.8 custom-call.37
  813.8 11.7 cholesky.519
  838.3 39.3 %custom-call.38 = f32[4,128,128]{1,2,0:T(8,128)S(1)} custom-call(f32[4,128,128]{2,1,0:T(8,128)S(1)} %get-tuple-element.33), custom_call_target="InvertDiagBlocksLowerTriangular" | custom-call | tf_op jit(solution)/shard_map/jit(_solve_triangular)/triangular_solve | solution.py:40
  884.9 48.4 %all-reduce.17.cloned.1.call-done = f32[512,512]{0,1:T(8,128)} async-done(((f32[512,512]{0,1:T(8,128)}), f32[512,512]{0,1:T(8,128)}) %all-reduce.17.cloned.1.call-update) | async-done | bytes 1048592 | tf_op jit(solution)/shard_map/psum | solution.py:10
  937.8 60.8 %all-reduce.27.cloned.1.call-done = (f32[512,512]{1,0:T(8,128)}, f32[512,512]{0,1:T(8,128)}) async-done(((f32[512,512]{1,0:T(8,128)}, f32[512,512]{0,1:T(8,128)}), (f32[512,512]{1,0:T(8,128)}, f32[512,512]{0,1:T(8,128)})) %all-reduce.27.cloned.1.call-update) | async-done | bytes 2097168 | tf_op jit(solution)/shard_map/psum | solution.py:45
  1006.3 11.7 cholesky.534
  1018.2 9.8 custom-call.39
  1030.6 11.9 cholesky.553
  1043.8 9.8 custom-call.40
  1055.2 11.7 cholesky.574
  1067.6 9.8 custom-call.41
  1078.8 12.1 cholesky.591
  1095.2 11.4 while.9
  1106.6 39.3 %custom-call.42 = f32[4,128,128]{1,2,0:T(8,128)S(1)} custom-call(f32[4,128,128]{2,1,0:T(8,128)S(1)} %get-tuple-element.34), custom_call_target="InvertDiagBlocksLowerTriangular" | custom-call | tf_op jit(solution)/shard_map/jit(_solve_triangular)/triangular_solve | solution.py:40
  1159.0 48.2 %all-reduce.19.cloned.1.call-done = f32[512,512]{0,1:T(8,128)} async-done(((f32[512,512]{0,1:T(8,128)}), f32[512,512]{0,1:T(8,128)}) %all-reduce.19.cloned.1.call-update) | async-done | bytes 1048592 | tf_op jit(solution)/shard_map/psum | solution.py:10
  1211.5 61.1 %all-reduce.25.cloned.1.call-done = (f32[512,512]{1,0:T(8,128)}, f32[512,512]{0,1:T(8,128)}) async-done(((f32[512,512]{1,0:T(8,128)}, f32[512,512]{0,1:T(8,128)}), (f32[512,512]{1,0:T(8,128)}, f32[512,512]{0,1:T(8,128)})) %all-reduce.25.cloned.1.call-update) | async-done | bytes 2097168 | tf_op jit(solution)/shard_map/psum | solution.py:45
  1280.2 11.7 cholesky.606
  1292.1 9.8 custom-call.43
  1304.5 11.9 cholesky.625
  1317.7 9.8 custom-call.44
  1329.1 11.7 cholesky.646
  1341.5 9.8 custom-call.45
  1352.8 12.1 cholesky.663
  1369.2 11.4 while.10
  1380.5 39.3 %custom-call.46 = f32[4,128,128]{1,2,0:T(8,128)S(1)} custom-call(f32[4,128,128]{2,1,0:T(8,128)S(1)} %get-tuple-element.35), custom_call_target="InvertDiagBlocksLowerTriangular" | custom-call | tf_op jit(solution)/shard_map/jit(_solve_triangular)/triangular_solve | solution.py:40
  1433.1 48.0 %all-reduce.21.cloned.1.call-done = f32[512,512]{0,1:T(8,128)} async-done(((f32[512,512]{0,1:T(8,128)}), f32[512,512]{0,1:T(8,128)}) %all-reduce.21.cloned.1.call-update) | async-done | bytes 1048592 | tf_op jit(solution)/shard_map/psum | solution.py:10
  1485.2 61.3 %all-reduce.23.cloned.1.call-done = (f32[512,512]{1,0:T(8,128)}, f32[512,512]{0,1:T(8,128)}) async-done(((f32[512,512]{1,0:T(8,128)}, f32[512,512]{0,1:T(8,128)}), (f32[512,512]{1,0:T(8,128)}, f32[512,512]{0,1:T(8,128)})) %all-reduce.23.cloned.1.call-update) | async-done | bytes 2097168 | tf_op jit(solution)/shard_map/psum | solution.py:45
  1554.2 11.7 cholesky.678
  1567.0 10.0 custom-call.47
  1580.2 11.7 cholesky.697
  1606.0 11.7 cholesky.718
  1619.1 10.2 custom-call.49
  1631.5 11.7 cholesky.735
  1650.2 13.7 while.11
  1663.9 40.1 %custom-call.50 = f32[4,128,128]{1,2,0:T(8,128)S(1)} custom-call(f32[4,128,128]{2,1,0:T(8,128)} %get-tuple-element.36), custom_call_target="InvertDiagBlocksLowerTriangular" | custom-call | tf_op jit(solution)/shard_map/jit(_solve_triangular)/triangular_solve | solution.py:40
  (229 shorter events, 202.7 us)
Async XLA Ops:
  6.5 588.5 %copy-start = (f32[512,512]{1,0:T(8,128)S(1)}, f32[512,512]{1,0:T(8,128)}, u32[]{:S(2)}) copy-start(f32[512,512]{1,0:T(8,128)} %param.6) | copy-start | bytes 3145732
  6.5 93.6 %all-gather.3.cloned.1.call-start = ((), (), s32[]{:S(2)}) async-start(), calls=%async_computation.2 | async-start | bytes 10485760 | tf_op jit(solution)/shard_map/all_gather | solution.py:59
  9.8 389.6 %all-reduce.13.cloned.1.call-start = ((), (), s32[]{:S(2)}) async-start(), calls=%async_computation.3 | async-start | bytes 16777216 | tf_op jit(solution)/shard_map/psum | solution.py:10
  108.4 334.3 %reduce-scatter.3.cloned.1.call-start = ((), (), s32[]{:S(2)}) async-start(), calls=%async_computation.4 | async-start | bytes 6291456 | tf_op jit(solution)/shard_map/reduce_scatter | solution.py:61
  431.5 163.5 %all-gather.5.cloned.1.call-start = ((), (), s32[]{:S(2)}) async-start(), calls=%async_computation.5 | async-start | bytes 10485760 | tf_op jit(solution)/shard_map/all_gather | solution.py:73
  442.7 239.1 %reduce-scatter.5.cloned.1.call-start = ((), (), s32[]{:S(2)}) async-start(), calls=%async_computation.6 | async-start | bytes 9437184 | tf_op jit(solution)/shard_map/reduce_scatter | solution.py:28
  612.2 131.0 %all-reduce.15.cloned.1.call-start = ((), (), s32[]{:S(2)}) async-start(), calls=%async_computation.7 | async-start | bytes 2097152 | tf_op jit(solution)/shard_map/psum | solution.py:37
  681.8 195.8 %copy-start.2 = (f32[512,512]{0,1:T(8,128)S(1)}, f32[512,512]{0,1:T(8,128)}, u32[]{:S(2)}) copy-start(f32[512,512]{0,1:T(8,128)} %reduce-scatter.5.cloned.1.call-done) | copy-start | bytes 3145732
  686.3 247.0 %all-reduce.17.cloned.1.call-start = ((), (), s32[]{:S(2)}) async-start(), calls=%async_computation.8 | async-start | bytes 2097152 | tf_op jit(solution)/shard_map/psum | solution.py:10
  882.0 116.7 %all-reduce.27.cloned.1.call-start = ((), (), s32[]{:S(2)}) async-start(), calls=%async_computation.13 | async-start | bytes 4194304 | tf_op jit(solution)/shard_map/psum | solution.py:45
  937.4 269.8 %all-reduce.19.cloned.1.call-start = ((), (), s32[]{:S(2)}) async-start(), calls=%async_computation.9 | async-start | bytes 2097152 | tf_op jit(solution)/shard_map/psum | solution.py:10
  998.7 147.3 %copy-start.4 = (f32[512,512]{1,0:T(8,128)S(1)}, f32[512,512]{1,0:T(8,128)}, u32[]{:S(2)}) copy-start(f32[512,512]{1,0:T(8,128)} %get-tuple-element.73) | copy-start | bytes 3145732
  1005.4 1.0 copy-start.6
  1156.1 116.5 %all-reduce.25.cloned.1.call-start = ((), (), s32[]{:S(2)}) async-start(), calls=%async_computation.12 | async-start | bytes 4194304 | tf_op jit(solution)/shard_map/psum | solution.py:45
  1211.3 269.9 %all-reduce.21.cloned.1.call-start = ((), (), s32[]{:S(2)}) async-start(), calls=%async_computation.10 | async-start | bytes 2097152 | tf_op jit(solution)/shard_map/psum | solution.py:10
  1272.6 147.3 %copy-start.5 = (f32[512,512]{1,0:T(8,128)S(1)}, f32[512,512]{1,0:T(8,128)}, u32[]{:S(2)}) copy-start(f32[512,512]{1,0:T(8,128)} %get-tuple-element.71) | copy-start | bytes 3145732
  1279.3 1.0 copy-start.7
  1430.1 116.5 %all-reduce.23.cloned.1.call-start = ((), (), s32[]{:S(2)}) async-start(), calls=%async_computation.11 | async-start | bytes 4194304 | tf_op jit(solution)/shard_map/psum | solution.py:45
  1546.5 157.5 %copy-start.3 = (f32[512,512]{1,0:T(8,128)S(1)}, f32[512,512]{1,0:T(8,128)}, u32[]{:S(2)}) copy-start(f32[512,512]{1,0:T(8,128)} %get-tuple-element.69) | copy-start | bytes 3145732
  1553.2 1.0 copy-start.8
  1647.0 67.5 %copy-start.1 = (f32[512,512]{1,0:T(8,128)S(1)}, f32[512,512]{1,0:T(8,128)}, u32[]{:S(2)}) copy-start(f32[512,512]{1,0:T(8,128)} %param.6) | copy-start | bytes 3145732
Sparse Core Ops, SparseCore 0:
  9.9 90.1 all-gather.2
  108.5 290.8 all-reduce.12
  431.7 10.9 reduce-scatter.2
  444.1 150.8 all-gather.4
  612.3 69.4 reduce-scatter.4
  686.4 56.6 all-reduce.14
  882.1 51.1 all-reduce.16
  937.5 61.1 all-reduce.26
  1156.2 50.9 all-reduce.18
  1211.4 61.1 all-reduce.24
  1430.2 50.9 all-reduce.20
  1485.3 61.1 all-reduce.22
where the time goes:
time: 1730 us; the launch traced here: 1720 us
  waiting for transfers between devices  998 us (58%)
  other arithmetic  500 us (29%)
  matrix products  136 us (8%)
  local copies, waits for them, and re-layouts  59.8 us (3%)
  between operations  24.6 us (1%)
    psum x4, waiting for transfers between devices, spread(): return lax.psum(jnp.where(mine, x, jnp.zeros_like(x)), axis)  436 us
    another operation x59, other arithmetic, orthonormalize(): factor = jnp.linalg.cholesky(gram_matrix)  319 us
    psum x3, waiting for transfers between devices, orthonormalize(): lax.psum((cross(chosen, current), cross(current, current)), ('col', 'laye...  183 us
    another operation x9, other arithmetic, orthonormalize(): jax.scipy.linalg.solve_triangular(factor, current.T, lower=True)  163 us
    all_gather x1, waiting for transfers between devices, shards(): rho_slab = lax.all_gather(rho_part, 'row', axis=1, tiled=True)  152 us
    all_gather x1, waiting for transfers between devices, shards(): own_rows = lax.all_gather(own_slice, 'col', axis=1, tiled=True)  90.3 us
    reduce_scatter x1, waiting for transfers between devices, apply_density(): lax.psum_scatter(cross(rho_slab, basis_block), ('col', 'layer'), scatter_...  69.6 us
    psum x1, waiting for transfers between devices, orthonormalize(): gram_matrix = lax.psum(cross(current, current), ('col', 'layer'))  56.3 us
  transfers between devices with their start and end apart: 12, of which 12 were waited for; matrix products, arithmetic and copies ran while one was open for 0% of the time, Pallas kernels for 0%

commit v1 on v0

--- a/solution.py
+++ b/solution.py
@@ -43,7 +43,7 @@
             chosen = spread(current, "row", panel_index)
             later = panel_owner > panel_index
             correlation, square = lax.psum(
-                (cross(chosen, current), cross(current, current)), ("col", "layer")
+                lax.psum((cross(chosen, current), cross(current, current)), "col"), "layer"
             )
             current = jnp.where(later, current - times(chosen, correlation), current)
             gram_matrix = jnp.where(later, square - cross(correlation, correlation), square)

time: 1730 us -> 1830 us (1.058)
  waiting for transfers between devices: 998 us -> 1100 us
    psum x3 -> x6, waiting for transfers between devices: 183 us -> 277 us  [the longest x3 206 us: orthonormalize(): lax.psum((cross(chosen, current), cross(current, current)), 'col')]
  transfers between devices with their start and end apart: 12 -> 15, of which waited for: 12 -> 15; matrix products, arithmetic and copies ran while one was open for 0% -> 0% of each run, Pallas kernels for 0% -> 0%
where the time goes in v1:
time: 1830 us; the launch traced here: 1820 us
  waiting for transfers between devices  1100 us (60%)
  other arithmetic  500 us (27%)
  matrix products  137 us (7%)
  local copies, waits for them, and re-layouts  59.8 us (3%)
  between operations  24.6 us (1%)
    psum x4, waiting for transfers between devices, spread(): return lax.psum(jnp.where(mine, x, jnp.zeros_like(x)), axis)  440 us
    another operation x59, other arithmetic, orthonormalize(): factor = jnp.linalg.cholesky(gram_matrix)  319 us
    psum x3, waiting for transfers between devices, orthonormalize(): lax.psum((cross(chosen, current), cross(current, current)), 'col')  206 us
    another operation x9, other arithmetic, orthonormalize(): jax.scipy.linalg.solve_triangular(factor, current.T, lower=True)  163 us
    all_gather x1, waiting for transfers between devices, shards(): rho_slab = lax.all_gather(rho_part, 'row', axis=1, tiled=True)  152 us
    all_gather x1, waiting for transfers between devices, shards(): own_rows = lax.all_gather(own_slice, 'col', axis=1, tiled=True)  90.3 us
    psum x3, waiting for transfers between devices, orthonormalize(): lax.psum(lax.psum((cross(chosen, current), cross(current, current)), 'col...  70.3 us
    reduce_scatter x1, waiting for transfers between devices, apply_density(): lax.psum_scatter(cross(rho_slab, basis_block), ('col', 'layer'), scatter_...  69.6 us
  transfers between devices with their start and end apart: 15, of which 15 were waited for; matrix products, arithmetic and copies ran while one was open for 0% of the time, Pallas kernels for 0%

profile of v1, /device:TPU:0, one launch (start us, length us, event | category | flops | bytes accessed | tf_op | source)
XLA Modules:
  0.0 1819.7 jit_solution(1168757772040982731)
XLA Ops:
  9.9 90.3 %all-gather.3.cloned.1.call-done = f32[1024,2048]{1,0:T(8,128)} async-done(((f32[1024,512]{1,0:T(8,128)}), f32[1024,2048]{1,0:T(8,128)}) %all-gather.3.cloned.1.call-update) | async-done | bytes 8388624 | tf_op jit(solution)/shard_map/all_gather | solution.py:59
  108.5 290.9 %all-reduce.19.cloned.1.call-done = f32[1024,2048]{1,0:T(8,128)} async-done(((f32[1024,2048]{1,0:T(8,128)}), f32[1024,2048]{1,0:T(8,128)}) %all-reduce.19.cloned.1.call-update) | async-done | bytes 8388624 | tf_op jit(solution)/shard_map/psum | solution.py:10
  399.4 32.1 %fusion.156 = f32[1024,1024]{1,0:T(8,128)} fusion(f32[1024,2048]{1,0:T(8,128)} %all-reduce.19.cloned.1.call-done, f32[1024,2048]{1,0:T(8,128)} %all-gather.3.cloned.1.call-done), kind=kOutput, calls=%fused_computation.284 | convolution fusion | flops 25769803776 | bytes 20971520 | tf_op jit(solution)/shard_map/dot_general | solution.py:62
  431.6 11.1 reduce-scatter.3.cloned.1.call-done
  443.0 152.1 %all-gather.5.cloned.1.call-done = f32[512,4096]{1,0:T(8,128)} async-done(((f32[512,1024]{1,0:T(8,128)}), f32[512,4096]{1,0:T(8,128)}) %all-gather.5.cloned.1.call-update) | async-done | bytes 8388624 | tf_op jit(solution)/shard_map/all_gather | solution.py:73
  595.1 17.1 fusion.157
  612.2 69.6 %reduce-scatter.5.cloned.1.call-done = f32[512,512]{0,1:T(8,128)} async-done(((f32[4096,512]{0,1:T(8,128)}), f32[512,512]{0,1:T(8,128)}) %reduce-scatter.5.cloned.1.call-update) | async-done | bytes 1048592 | tf_op jit(solution)/shard_map/reduce_scatter | solution.py:28
  686.6 56.6 %all-reduce.21.cloned.1.call-done = f32[512,512]{0,1:T(8,128)} async-done(((f32[512,512]{0,1:T(8,128)}), f32[512,512]{0,1:T(8,128)}) %all-reduce.21.cloned.1.call-update) | async-done | bytes 1048592 | tf_op jit(solution)/shard_map/psum | solution.py:37
  746.2 11.7 cholesky.462
  758.0 9.8 custom-call.35
  768.6 11.7 cholesky.481
  780.3 10.2 custom-call.36
  791.2 11.7 cholesky.502
  814.1 11.7 cholesky.519
  838.5 39.3 %custom-call.38 = f32[4,128,128]{1,2,0:T(8,128)S(1)} custom-call(f32[4,128,128]{2,1,0:T(8,128)S(1)} %get-tuple-element.33), custom_call_target="InvertDiagBlocksLowerTriangular" | custom-call | tf_op jit(solution)/shard_map/jit(_solve_triangular)/triangular_solve | solution.py:40
  885.2 48.3 %all-reduce.23.cloned.1.call-done = f32[512,512]{0,1:T(8,128)} async-done(((f32[512,512]{0,1:T(8,128)}), f32[512,512]{0,1:T(8,128)}) %all-reduce.23.cloned.1.call-update) | async-done | bytes 1048592 | tf_op jit(solution)/shard_map/psum | solution.py:10
  937.7 68.9 %all-reduce.33.cloned.1.call-done = (f32[512,512]{1,0:T(8,128)}, f32[512,512]{0,1:T(8,128)}) async-done(((f32[512,512]{1,0:T(8,128)}, f32[512,512]{0,1:T(8,128)}), (f32[512,512]{1,0:T(8,128)}, f32[512,512]{0,1:T(8,128)})) %all-reduce.33.cloned.1.call-update) | async-done | bytes 2097168 | tf_op jit(solution)/shard_map/psum | solution.py:46
  1006.8 23.5 %all-reduce.39.cloned.1.call-done = (f32[512,512]{1,0:T(8,128)}, f32[512,512]{0,1:T(8,128)}) async-done(((f32[512,512]{1,0:T(8,128)}, f32[512,512]{0,1:T(8,128)}), (f32[512,512]{1,0:T(8,128)}, f32[512,512]{0,1:T(8,128)})) %all-reduce.39.cloned.1.call-update) | async-done | bytes 2097168 | tf_op jit(solution)/shard_map/psum | solution.py:45
  1038.0 11.7 cholesky.534
  1049.9 9.8 custom-call.39
  1062.2 12.2 cholesky.553
  1075.7 9.8 custom-call.40
  1087.1 11.7 cholesky.574
  1099.5 9.8 custom-call.41
  1110.8 11.9 cholesky.591
  1126.9 11.4 while.9
  1138.3 39.3 %custom-call.42 = f32[4,128,128]{1,2,0:T(8,128)S(1)} custom-call(f32[4,128,128]{2,1,0:T(8,128)S(1)} %get-tuple-element.34), custom_call_target="InvertDiagBlocksLowerTriangular" | custom-call | tf_op jit(solution)/shard_map/jit(_solve_triangular)/triangular_solve | solution.py:40
  1190.8 50.3 %all-reduce.25.cloned.1.call-done = f32[512,512]{0,1:T(8,128)} async-done(((f32[512,512]{0,1:T(8,128)}), f32[512,512]{0,1:T(8,128)}) %all-reduce.25.cloned.1.call-update) | async-done | bytes 1048592 | tf_op jit(solution)/shard_map/psum | solution.py:10
  1245.2 68.9 %all-reduce.31.cloned.1.call-done = (f32[512,512]{1,0:T(8,128)}, f32[512,512]{0,1:T(8,128)}) async-done(((f32[512,512]{1,0:T(8,128)}, f32[512,512]{0,1:T(8,128)}), (f32[512,512]{1,0:T(8,128)}, f32[512,512]{0,1:T(8,128)})) %all-reduce.31.cloned.1.call-update) | async-done | bytes 2097168 | tf_op jit(solution)/shard_map/psum | solution.py:46
  1314.5 23.2 %all-reduce.37.cloned.1.call-done = (f32[512,512]{1,0:T(8,128)}, f32[512,512]{0,1:T(8,128)}) async-done(((f32[512,512]{1,0:T(8,128)}, f32[512,512]{0,1:T(8,128)}), (f32[512,512]{1,0:T(8,128)}, f32[512,512]{0,1:T(8,128)})) %all-reduce.37.cloned.1.call-update) | async-done | bytes 2097168 | tf_op jit(solution)/shard_map/psum | solution.py:45
  1345.4 11.7 cholesky.606
  1357.3 9.8 custom-call.43
  1369.6 11.9 cholesky.625
  1382.8 9.8 custom-call.44
  1394.2 11.7 cholesky.646
  1406.6 9.8 custom-call.45
  1417.9 12.1 cholesky.663
  1434.3 11.4 while.10
  1445.7 39.3 %custom-call.46 = f32[4,128,128]{1,2,0:T(8,128)S(1)} custom-call(f32[4,128,128]{2,1,0:T(8,128)S(1)} %get-tuple-element.35), custom_call_target="InvertDiagBlocksLowerTriangular" | custom-call | tf_op jit(solution)/shard_map/jit(_solve_triangular)/triangular_solve | solution.py:40
  1498.1 50.3 %all-reduce.27.cloned.1.call-done = f32[512,512]{0,1:T(8,128)} async-done(((f32[512,512]{0,1:T(8,128)}), f32[512,512]{0,1:T(8,128)}) %all-reduce.27.cloned.1.call-update) | async-done | bytes 1048592 | tf_op jit(solution)/shard_map/psum | solution.py:10
  1552.7 68.7 %all-reduce.29.cloned.1.call-done = (f32[512,512]{1,0:T(8,128)}, f32[512,512]{0,1:T(8,128)}) async-done(((f32[512,512]{1,0:T(8,128)}, f32[512,512]{0,1:T(8,128)}), (f32[512,512]{1,0:T(8,128)}, f32[512,512]{0,1:T(8,128)})) %all-reduce.29.cloned.1.call-update) | async-done | bytes 2097168 | tf_op jit(solution)/shard_map/psum | solution.py:46
  1621.4 23.6 %all-reduce.35.cloned.1.call-done = (f32[512,512]{1,0:T(8,128)}, f32[512,512]{0,1:T(8,128)}) async-done(((f32[512,512]{1,0:T(8,128)}, f32[512,512]{0,1:T(8,128)}), (f32[512,512]{1,0:T(8,128)}, f32[512,512]{0,1:T(8,128)})) %all-reduce.35.cloned.1.call-update) | async-done | bytes 2097168 | tf_op jit(solution)/shard_map/psum | solution.py:45
  1652.7 11.7 cholesky.678
  1678.6 11.9 cholesky.697
  1704.5 11.7 cholesky.718
  1729.7 11.9 cholesky.735
  1748.6 13.5 while.11
  1762.1 40.1 %custom-call.50 = f32[4,128,128]{1,2,0:T(8,128)S(1)} custom-call(f32[4,128,128]{2,1,0:T(8,128)} %get-tuple-element.36), custom_call_target="InvertDiagBlocksLowerTriangular" | custom-call | tf_op jit(solution)/shard_map/jit(_solve_triangular)/triangular_solve | solution.py:40
  (238 shorter events, 232.0 us)
Async XLA Ops:
  6.5 588.5 %copy-start = (f32[512,512]{1,0:T(8,128)S(1)}, f32[512,512]{1,0:T(8,128)}, u32[]{:S(2)}) copy-start(f32[512,512]{1,0:T(8,128)} %param.6) | copy-start | bytes 3145732
  6.5 93.6 %all-gather.3.cloned.1.call-start = ((), (), s32[]{:S(2)}) async-start(), calls=%async_computation.2 | async-start | bytes 10485760 | tf_op jit(solution)/shard_map/all_gather | solution.py:59
  9.8 389.6 %all-reduce.19.cloned.1.call-start = ((), (), s32[]{:S(2)}) async-start(), calls=%async_computation.3 | async-start | bytes 16777216 | tf_op jit(solution)/shard_map/psum | solution.py:10
  108.4 334.3 %reduce-scatter.3.cloned.1.call-start = ((), (), s32[]{:S(2)}) async-start(), calls=%async_computation.4 | async-start | bytes 6291456 | tf_op jit(solution)/shard_map/reduce_scatter | solution.py:61
  431.5 163.5 %all-gather.5.cloned.1.call-start = ((), (), s32[]{:S(2)}) async-start(), calls=%async_computation.5 | async-start | bytes 10485760 | tf_op jit(solution)/shard_map/all_gather | solution.py:73
  442.7 239.1 %reduce-scatter.5.cloned.1.call-start = ((), (), s32[]{:S(2)}) async-start(), calls=%async_computation.6 | async-start | bytes 9437184 | tf_op jit(solution)/shard_map/reduce_scatter | solution.py:28
  612.2 131.0 %all-reduce.21.cloned.1.call-start = ((), (), s32[]{:S(2)}) async-start(), calls=%async_computation.7 | async-start | bytes 2097152 | tf_op jit(solution)/shard_map/psum | solution.py:37
  681.8 196.0 %copy-start.2 = (f32[512,512]{0,1:T(8,128)S(1)}, f32[512,512]{0,1:T(8,128)}, u32[]{:S(2)}) copy-start(f32[512,512]{0,1:T(8,128)} %reduce-scatter.5.cloned.1.call-done) | copy-start | bytes 3145732
  686.3 247.2 %all-reduce.23.cloned.1.call-start = ((), (), s32[]{:S(2)}) async-start(), calls=%async_computation.8 | async-start | bytes 2097152 | tf_op jit(solution)/shard_map/psum | solution.py:10
  882.2 124.3 %all-reduce.33.cloned.1.call-start = ((), (), s32[]{:S(2)}) async-start(), calls=%async_computation.13 | async-start | bytes 4194304 | tf_op jit(solution)/shard_map/psum | solution.py:46
  937.6 92.7 %all-reduce.39.cloned.1.call-start = ((), (), s32[]{:S(2)}) async-start(), calls=%async_computation.16 | async-start | bytes 4194304 | tf_op jit(solution)/shard_map/psum | solution.py:45
  1006.5 234.5 %all-reduce.25.cloned.1.call-start = ((), (), s32[]{:S(2)}) async-start(), calls=%async_computation.9 | async-start | bytes 2097152 | tf_op jit(solution)/shard_map/psum | solution.py:10
  1030.3 147.3 %copy-start.4 = (f32[512,512]{1,0:T(8,128)S(1)}, f32[512,512]{1,0:T(8,128)}, u32[]{:S(2)}) copy-start(f32[512,512]{1,0:T(8,128)} %get-tuple-element.79) | copy-start | bytes 3145732
  1037.0 1.0 copy-start.6
  1187.8 126.2 %all-reduce.31.cloned.1.call-start = ((), (), s32[]{:S(2)}) async-start(), calls=%async_computation.12 | async-start | bytes 4194304 | tf_op jit(solution)/shard_map/psum | solution.py:46
  1245.1 92.6 %all-reduce.37.cloned.1.call-start = ((), (), s32[]{:S(2)}) async-start(), calls=%async_computation.15 | async-start | bytes 4194304 | tf_op jit(solution)/shard_map/psum | solution.py:45
  1314.1 234.3 %all-reduce.27.cloned.1.call-start = ((), (), s32[]{:S(2)}) async-start(), calls=%async_computation.10 | async-start | bytes 2097152 | tf_op jit(solution)/shard_map/psum | solution.py:10
  1337.7 147.3 %copy-start.5 = (f32[512,512]{1,0:T(8,128)S(1)}, f32[512,512]{1,0:T(8,128)}, u32[]{:S(2)}) copy-start(f32[512,512]{1,0:T(8,128)} %get-tuple-element.77) | copy-start | bytes 3145732
  1344.4 1.0 copy-start.7
  1495.2 126.2 %all-reduce.29.cloned.1.call-start = ((), (), s32[]{:S(2)}) async-start(), calls=%async_computation.11 | async-start | bytes 4194304 | tf_op jit(solution)/shard_map/psum | solution.py:46
  1552.5 92.6 %all-reduce.35.cloned.1.call-start = ((), (), s32[]{:S(2)}) async-start(), calls=%async_computation.14 | async-start | bytes 4194304 | tf_op jit(solution)/shard_map/psum | solution.py:45
  1645.0 157.2 %copy-start.3 = (f32[512,512]{1,0:T(8,128)S(1)}, f32[512,512]{1,0:T(8,128)}, u32[]{:S(2)}) copy-start(f32[512,512]{1,0:T(8,128)} %get-tuple-element.75) | copy-start | bytes 3145732
  1651.7 1.0 copy-start.8
  1745.4 67.4 %copy-start.1 = (f32[512,512]{1,0:T(8,128)S(1)}, f32[512,512]{1,0:T(8,128)}, u32[]{:S(2)}) copy-start(f32[512,512]{1,0:T(8,128)} %param.6) | copy-start | bytes 3145732
Sparse Core Ops, SparseCore 0:
  9.9 90.1 all-gather.2
  108.5 290.8 all-reduce.18
  431.7 10.9 reduce-scatter.2
  444.1 150.8 all-gather.4
  612.3 69.4 reduce-scatter.4
  686.5 56.7 all-reduce.20
  882.4 51.1 all-reduce.22
  937.7 68.7 all-reduce.32
  1008.9 21.3 all-reduce.38
  1188.0 53.0 all-reduce.24
  1245.3 68.7 all-reduce.30
  1316.3 21.3 all-reduce.36
  1495.3 53.0 all-reduce.26
  1552.6 68.7 all-reduce.28
  1623.6 21.3 all-reduce.34
